TPU v7x, 32 devices: a whole 2x2x4 slice. The times are simulated.
32 devices in a mesh: blk: 4 (over y, core), row: 8 (over z, x).
Axes of the slice: x: 2, y: 2, z: 4, core: 2. Of those that a mesh axis runs over, the one named last changes fastest.
Arguments:
- factor: float32 [4, 1536, 1536], P('blk', 'row'), may hold values from -1 to 1, as said below
- coupling: float32 [4, 128, 128], P('blk'), may hold values from -1.5 to 1.5
- right_side: float32 [4, 1536, 128], P('blk', 'row'), may hold values from -6 to 6
Outputs:
- inverse: float32 [4, 1536, 1536], P('blk', 'row')
- solution: float32 [4, 1536, 128], P('blk', 'row')
Inputs may be any that keep to these rules, and one draw needn't show every extreme that they name: Each factor[b] has ones on its diagonal and zeros above it.
All inputs are finite; a program needn't handle non-finite values.
Results may differ from a plain program's by a relative error of at most 0.0003.
Values sent between devices are 32-bit elements; how exact they have to be, the bound alone decides.
No kernel may reach another device: no remote copies, remote signals or barrier semaphores. Data moves between devices by JAX's collectives and lax.ppermute only.
A program may use at most 128 MiB of HBM per device.

v0:
```python
import jax
import jax.numpy as jnp
from jax import lax
from jax.sharding import PartitionSpec as P

highest = lax.Precision.HIGHEST


def swapped(block, axis, bit):
    count = lax.axis_size(axis)
    route = []
    for low in range(count):
        high = low | 1 << bit
        if high != low and high < count:
            route += [(low, high), (high, low)]
    return lax.ppermute(block, axis, route)


def from_behind(block, axis, distance):
    devices = range(lax.axis_size(axis))
    route = [(i - distance, i) for i in devices if i - distance in devices]
    return lax.ppermute(block, axis, route)


def from_root(value, axis, root):
    mine = lax.axis_index(axis) == root
    return lax.psum(jnp.where(mine, value, jnp.zeros_like(value)), axis)


def entering(value, axis, join, neutral):
    count, mine = (lax.axis_size(axis), lax.axis_index(axis))
    pieces = jax.tree.map(lambda part: lax.all_gather(part, axis), value)
    so_far = jax.tree.map(
        lambda part, zero: jnp.full_like(part, 0) + jnp.asarray(zero, part.dtype), value, neutral
    )

    def turn(position, so_far):
        longer = join(so_far, jax.tree.map(lambda part: part[position], pieces))
        return jax.tree.map(lambda new, old: jnp.where(position < mine, new, old), longer, so_far)

    return lax.fori_loop(0, count - 1, turn, so_far)


def stacked(own_rows, partner, my_index, bit_index):
    is_high = jnp.bitwise_and(jnp.right_shift(my_index, bit_index), 1) == 1
    return jnp.where(
        is_high,
        jnp.concatenate([partner, own_rows], axis=1),
        jnp.concatenate([own_rows, partner], axis=1),
    )


def unit_solve(matrix, target, transposed):
    return jax.scipy.linalg.solve_triangular(
        matrix, target, trans=transposed, lower=True, unit_diagonal=True
    )


def sweep_local(incoming, tail_gain, tail_term):
    current = incoming
    previous = [current]
    current = tail_term[0] + jnp.dot(tail_gain[0], current, precision=highest)
    return (current, jnp.stack(previous))


def compose(earlier, later):
    return (
        jnp.dot(later[0], earlier[0], precision=highest),
        jnp.dot(later[0], earlier[1], precision=highest) + later[1],
    )


def on_device(factor, coupling, right_side):
    row_count = lax.axis_size("row")
    my_index = lax.axis_index("row")
    local_blocks, panel_rows, block_order = factor.shape
    band_width = coupling.shape[1]
    levels = row_count.bit_length() - 1
    identity = jnp.eye(panel_rows, dtype=jnp.float32)
    first_col = my_index * panel_rows
    diagonal = lax.dynamic_slice_in_dim(factor, first_col, panel_rows, 2)
    base_inverse = jax.vmap(lambda matrix: unit_solve(matrix, identity, 0))(diagonal)
    inverse = lax.dynamic_update_slice_in_dim(jnp.zeros_like(factor), base_inverse, first_col, 2)
    for section_level in range(levels):
        half_size = 1 << section_level
        span_width = half_size * panel_rows
        offset = my_index % (2 * half_size)
        group_first = (my_index - offset) * panel_rows
        is_lower = offset >= half_size
        inverse_piece = lax.dynamic_slice_in_dim(inverse, group_first, span_width, 2)
        factor_piece = lax.dynamic_slice_in_dim(factor, group_first, span_width, 2)
        assembled = jnp.where(is_lower, factor_piece, inverse_piece)
        for bit_index in range(section_level):
            partner = swapped(assembled, "row", bit_index)
            assembled = stacked(assembled, partner, my_index, bit_index)
        leading = from_behind(assembled, "row", half_size)
        corner_block = lax.dynamic_slice_in_dim(inverse, group_first + span_width, span_width, 2)
        coupled = jnp.einsum("nrw,nwv->nrv", corner_block, assembled, precision=highest)
        new_rows = -jnp.einsum("nrw,nwv->nrv", coupled, leading, precision=highest)
        inverse = jnp.where(
            is_lower, lax.dynamic_update_slice_in_dim(inverse, new_rows, group_first, 2), inverse
        )
    direct = jnp.einsum(
        "nrb,nbk->nrk",
        inverse,
        lax.all_gather(right_side, "row", axis=1, tiled=True),
        precision=highest,
    )
    gain_cols = -jnp.einsum("nrb,nbc->nrc", inverse[:, :, :band_width], coupling, precision=highest)
    tail_rows = jnp.concatenate(
        [gain_cols[:, panel_rows - band_width :, :], direct[:, panel_rows - band_width :, :]],
        axis=2,
    )
    tail_rows = from_root(tail_rows, "row", row_count - 1)
    tail_gain = tail_rows[:, :, :band_width]
    tail_term = tail_rows[:, :, band_width:]
    zero_tail = jnp.zeros((band_width, right_side.shape[2]), jnp.float32)
    matrix = jnp.eye(band_width, dtype=jnp.float32)
    shifted = zero_tail
    matrix, shifted = compose((matrix, shifted), (tail_gain[0], tail_term[0]))
    identity_map = (jnp.eye(band_width, dtype=jnp.float32), zero_tail)
    prefix_map = entering((matrix, shifted), "blk", compose, identity_map)
    incoming = prefix_map[1]
    final_tail, previous = sweep_local(incoming, tail_gain, tail_term)
    solution = direct + jnp.einsum("nrc,nck->nrk", gain_cols, previous, precision=highest)
    return (inverse, solution)


def solution(mesh):
    in_specs = (P("blk", "row", None), P("blk", None, None), P("blk", "row", None))
    out_specs = (P("blk", "row", None), P("blk", "row", None))
    return jax.shard_map(
        on_device, mesh=mesh, in_specs=in_specs, out_specs=out_specs, check_vma=False
    )
```

profile of v0, /device:TPU:30, one launch (start us, length us, event | category | flops | bytes accessed | tf_op | source)
XLA Modules:
  0.0 345.4 jit_solution(17582094733105799554)
XLA Ops:
  7.2 0.0 copy-start
  7.2 0.0 all-reduce.4.cloned.1.call-start
  7.3 1.1 convert_add_fusion
  8.4 0.1 fusion.54
  8.5 19.7 %custom-call.4 = f32[1,2,128,128]{2,3,1,0:T(8,128)S(1)} custom-call(f32[1,2,128,128]{3,2,1,0:T(8,128)S(1)} %pad_maximum_fusion.1), custom_call_target="InvertDiagBlocksLowerTriangular" | custom-call | tf_op jit(solution)/shard_map/vmap(jit(_solve_triangular))/triangular_solve | solution.py:54
  28.2 0.3 fusion.53
  28.5 0.3 fusion.34
  28.8 0.3 convolution_bitcast_fusion
  29.2 0.0 copy-start.4
  29.2 0.1 copy.6
  29.3 0.1 broadcast_in_dim.11
  29.4 1.2 dynamic_update_slice.2
  30.6 0.0 copy-done.4
  30.6 0.2 dynamic-slice_select_fusion.2
  30.8 1.3 collective-permute-start
  32.1 0.4 fusion.49
  32.5 6.8 %collective-permute-done = f32[1,192,192]{2,1,0:T(8,128)S(1)} collective-permute-done((f32[1,192,192]{2,1,0:T(8,128)S(1)}, f32[1,192,192]{2,1,0:T(8,128)S(1)}, u32[]{:S(2)}, u32[]{:S(2)}) %collective-permute-start) | collective-permute-done | bytes 147488 | tf_op jit(solution)/shard_map/ppermute | solution.py:22
  39.4 0.3 fusion.31
  39.7 1.2 select_n.205
  40.9 0.2 dynamic-slice_select_fusion.1
  41.2 1.6 collective-permute-start.1
  42.8 6.3 %collective-permute-done.1 = f32[1,192,384]{2,1,0:T(8,128)S(1)} collective-permute-done((f32[1,192,384]{2,1,0:T(8,128)S(1)}, f32[1,192,384]{2,1,0:T(8,128)S(1)}, u32[]{:S(2)}, u32[]{:S(2)}) %collective-permute-start.1) | collective-permute-done | bytes 294944 | tf_op jit(solution)/shard_map/ppermute | solution.py:16
  49.1 0.7 copy-done.5
  49.8 0.9 maximum_select_fusion.7
  50.7 1.3 collective-permute-start.2
  52.0 1.9 fusion.36
  53.8 12.3 %collective-permute-done.2 = f32[1,384,384]{2,1,0:T(8,128)S(1)} collective-permute-done((f32[1,384,384]{2,1,0:T(8,128)}, f32[1,384,384]{2,1,0:T(8,128)S(1)}, u32[]{:S(2)}, u32[]{:S(2)}) %collective-permute-start.2) | collective-permute-done | bytes 589856 | tf_op jit(solution)/shard_map/ppermute | solution.py:22
  66.1 0.8 fusion.30
  66.9 3.3 select_n.216
  70.2 0.4 dynamic-slice_select_fusion
  70.5 1.6 collective-permute-start.3
  72.2 10.9 %collective-permute-done.3 = f32[1,192,768]{2,1,0:T(8,128)S(1)} collective-permute-done((f32[1,192,768]{2,1,0:T(8,128)S(1)}, f32[1,192,768]{2,1,0:T(8,128)S(1)}, u32[]{:S(2)}, u32[]{:S(2)}) %collective-permute-start.3) | collective-permute-done | bytes 589856 | tf_op jit(solution)/shard_map/ppermute | solution.py:16
  83.1 1.2 maximum_select_fusion.3
  84.3 0.0 copy-done.3
  84.3 1.4 collective-permute-start.4
  85.8 1.4 maximum_select_fusion.4
  87.1 21.8 %collective-permute-done.4 = f32[1,384,768]{2,1,0:T(8,128)} collective-permute-done((f32[1,384,768]{2,1,0:T(8,128)}, f32[1,384,768]{2,1,0:T(8,128)}, u32[]{:S(2)}, u32[]{:S(2)}) %collective-permute-start.4) | collective-permute-done | bytes 1179680 | tf_op jit(solution)/shard_map/ppermute | solution.py:16
  108.9 3.3 maximum_select_fusion.2
  112.3 1.3 collective-permute-start.5
  113.6 0.0 copy-done.6
  113.6 123.3 %all_gather.15 = f32[1,1536,128]{2,1,0:T(8,128)} all-gather(f32[1,192,128]{2,1,0:T(8,128)S(1)} %copy-done.6), channel_id=1, replica_groups=mesh['blk'=4,'row'=8] {'row'}, dimensions={1}, use_global_device_ids=true | all-gather | bytes 884736 | tf_op jit(solution)/shard_map/all_gather | solution.py:106
  236.9 3.5 %fusion.8 = f32[192,768]{1,0:T(8,128)S(1)} fusion(f32[384,768]{1,0:T(8,128)S(1)} %maximum_select_fusion.4, f32[384,768]{1,0:T(8,128)} %bitcast.21, pred[]{:T(512)S(6)} %eq.35, f32[1,192,1536]{2,1,0:T(8,128)S(1)} %select_n.216, s32[]{:T(128)S(6)} %select_n.219), kind=kOutput, calls=%fused_computation.10 | convolution fusion | flops 1360723968 | bytes 3538949 | tf_op jit(solution)/shard_map/nrw,nwv->nrv/dot_general | solution.py:98
  240.4 0.0 collective-permute-done.5
  240.4 3.4 fusion.22
  243.8 0.0 copy-start.2
  243.8 5.9 %select_n.231 = f32[1,192,1536]{2,1,0:T(8,128)S(1)} dynamic-update-slice(f32[1,192,1536]{2,1,0:T(8,128)S(1)} %select_n.216, f32[1,192,768]{2,1,0:T(8,128)S(1)} %fusion.22, s32[]{:T(128)} %constant.86.clone.1, s32[]{:T(128)} %constant.86.clone.1, s32[]{:T(128)S(6)} %select_n.222) | dynamic-update-slice | bytes 1179652 | tf_op jit(solution)/shard_map/jit(_where)/select_n | solution.py:100
  249.7 0.0 copy-done.2
  249.7 0.0 copy-start.1
  249.7 1.1 fusion.25
  250.8 0.0 copy-done
  250.8 0.2 convolution_negate_fusion.2
  251.1 0.0 copy-done.1
  251.1 0.7 maximum_select_fusion.8
  251.7 0.0 all-reduce.4.cloned.1.call-update
  251.8 71.4 %all-reduce.4.cloned.1.call-done = f32[1,128,256]{2,1,0:T(8,128)} async-done(((f32[1,128,256]{2,1,0:T(8,128)}), f32[1,128,256]{2,1,0:T(8,128)}) %all-reduce.4.cloned.1.call-update) | async-done | bytes 131088 | tf_op jit(solution)/shard_map/psum | solution.py:27
  323.2 1.0 fusion.56
  324.3 5.8 %all-gather = f32[512,128]{1,0:T(8,128)S(1)} all-gather(f32[128,128]{1,0:T(8,128)S(1)} %fusion.56), channel_id=2, replica_groups=mesh['blk'=4,'row'=8] {'blk'}, dimensions={0}, use_global_device_ids=true | all-gather | bytes 327680 | tf_op jit(solution)/shard_map/all_gather | solution.py:32
  330.0 1.1 convolution_add_fusion.2
  331.1 5.9 %all-gather.1 = f32[512,128]{1,0:T(8,128)S(1)} all-gather(f32[128,128]{1,0:T(8,128)S(1)} %convolution_add_fusion.2), channel_id=3, replica_groups=mesh['blk'=4,'row'=8] {'blk'}, dimensions={0}, use_global_device_ids=true | all-gather | bytes 327680 | tf_op jit(solution)/shard_map/all_gather | solution.py:32
  336.9 0.7 while.16
  337.0 0.2 fusion.76
  337.2 0.2 fusion.76
  337.5 0.2 fusion.76
  337.7 0.9 fusion.32
  (16 shorter events, 0.1 us)
Async XLA Ops:
  7.2 243.6 %copy-start = (f32[1,128,128]{2,1,0:T(8,128)S(1)}, f32[1,128,128]{2,1,0:T(8,128)}, u32[]{:S(2)}) copy-start(f32[1,128,128]{2,1,0:T(8,128)} %param.6) | copy-start | bytes 196612
  7.2 316.0 %all-reduce.4.cloned.1.call-start = ((), (), s32[]{:S(2)}) async-start(), calls=%async_computation | async-start | bytes 262144 | tf_op jit(solution)/shard_map/psum | solution.py:27
  29.2 1.4 copy-start.4
  30.8 8.5 %collective-permute-start = (f32[1,192,192]{2,1,0:T(8,128)S(1)}, f32[1,192,192]{2,1,0:T(8,128)S(1)}, u32[]{:S(2)}, u32[]{:S(2)}) collective-permute-start(f32[1,192,192]{2,1,0:T(8,128)S(1)} %dynamic-slice_select_fusion.2), channel_id=1, source_target_pairs={{0,1},{1,2},{2,3},{3,4},{4,5},{5,6},{6,7},{8,9},{9,10},{10,11},{11... | collective-permute-start | bytes 442376 | tf_op jit(solution)/shard_map/ppermute | solution.py:22
  41.2 8.0 %collective-permute-start.1 = (f32[1,192,384]{2,1,0:T(8,128)S(1)}, f32[1,192,384]{2,1,0:T(8,128)S(1)}, u32[]{:S(2)}, u32[]{:S(2)}) collective-permute-start(f32[1,192,384]{2,1,0:T(8,128)S(1)} %dynamic-slice_select_fusion.1), channel_id=1, source_target_pairs={{0,1},{1,0},{2,3},{3,2},{4,5},{5,4},{6,7},{7,6},{8,9},{9,8},{10,11... | collective-permute-start | bytes 884744 | tf_op jit(solution)/shard_map/ppermute | solution.py:16
  49.1 0.7 copy-start.5
  50.7 15.4 %collective-permute-start.2 = (f32[1,384,384]{2,1,0:T(8,128)}, f32[1,384,384]{2,1,0:T(8,128)S(1)}, u32[]{:S(2)}, u32[]{:S(2)}) collective-permute-start(f32[1,384,384]{2,1,0:T(8,128)} %maximum_select_fusion.7), channel_id=1, source_target_pairs={{0,2},{1,3},{2,4},{3,5},{4,6},{5,7},{8,10},{9,11},{10,12},{11,13},... | collective-permute-start | bytes 1769480 | tf_op jit(solution)/shard_map/ppermute | solution.py:22
  70.5 12.6 %collective-permute-start.3 = (f32[1,192,768]{2,1,0:T(8,128)S(1)}, f32[1,192,768]{2,1,0:T(8,128)S(1)}, u32[]{:S(2)}, u32[]{:S(2)}) collective-permute-start(f32[1,192,768]{2,1,0:T(8,128)S(1)} %dynamic-slice_select_fusion), channel_id=1, source_target_pairs={{0,1},{1,0},{2,3},{3,2},{4,5},{5,4},{6,7},{7,6},{8,9},{9,8},{10,11... | collective-permute-start | bytes 1769480 | tf_op jit(solution)/shard_map/ppermute | solution.py:16
  83.1 1.2 copy-start.3
  84.3 24.6 %collective-permute-start.4 = (f32[1,384,768]{2,1,0:T(8,128)}, f32[1,384,768]{2,1,0:T(8,128)}, u32[]{:S(2)}, u32[]{:S(2)}) collective-permute-start(f32[1,384,768]{2,1,0:T(8,128)} %maximum_select_fusion.3), channel_id=1, source_target_pairs={{0,2},{2,0},{1,3},{3,1},{4,6},{6,4},{5,7},{7,5},{8,10},{10,8},{9,1... | collective-permute-start | bytes 3538952 | tf_op jit(solution)/shard_map/ppermute | solution.py:16
  108.9 4.6 %copy-start.6 = (f32[1,192,128]{2,1,0:T(8,128)S(1)}, f32[1,192,128]{2,1,0:T(8,128)}, u32[]{:S(2)}) copy-start(f32[1,192,128]{2,1,0:T(8,128)} %param.7) | copy-start | bytes 294916
  112.3 128.1 %collective-permute-start.5 = (f32[1,768,768]{2,1,0:T(8,128)}, f32[1,768,768]{2,1,0:T(8,128)}, u32[]{:S(2)}, u32[]{:S(2)}) collective-permute-start(f32[1,768,768]{2,1,0:T(8,128)} %maximum_select_fusion.2), channel_id=1, source_target_pairs={{0,4},{1,5},{2,6},{3,7},{8,12},{9,13},{10,14},{11,15},{16,20},{17,... | collective-permute-start | bytes 7077896 | tf_op jit(solution)/shard_map/ppermute | solution.py:22
  243.8 5.9 %copy-start.2 = (f32[1,1536,128]{2,1,0:T(8,128)S(1)}, f32[1,1536,128]{2,1,0:T(8,128)}, u32[]{:S(2)}) copy-start(f32[1,1536,128]{2,1,0:T(8,128)} %all_gather.15) | copy-start | bytes 2359300
  249.7 1.4 copy-start.1
Sparse Core Ops, SparseCore 0:
  251.9 71.2 all-reduce.3
where the time goes:
time: 349 us; the launch traced here: 345 us
  blocking collectives  135 us (39%)
  waiting for transfers between devices  130 us (37%)
  other arithmetic  29.1 us (8%)
  matrix products  16 us (5%)
  between operations  14.5 us (4%)
  local copies, waits for them, and re-layouts  12.5 us (4%)
  starting transfers between devices  8.58 us (2%)
    all_gather x1, blocking collectives, on_device(): lax.all_gather(right_side, 'row', axis=1, tiled=True)  123 us
    psum x1, waiting for transfers between devices, from_root(): return lax.psum(jnp.where(mine, value, jnp.zeros_like(value)), axis)  71.4 us
    ppermute x3, waiting for transfers between devices, swapped(): return lax.ppermute(block, axis, route)  39.1 us
    another operation x8, other arithmetic, unit_solve(): jax.scipy.linalg.solve_triangular(matrix, target, trans=transposed, lower...  20.9 us
    ppermute x3, waiting for transfers between devices, from_behind(): return lax.ppermute(block, axis, route)  19.1 us
    all_gather x2, blocking collectives, entering(): pieces = jax.tree.map(lambda part: lax.all_gather(part, axis), value)  11.6 us
    select_n x3, local copies, waits for them, and re-layouts, on_device(): jnp.where(is_lower, lax.dynamic_update_slice_in_dim(inverse, new_rows, gr...  10.4 us
  transfers between devices with their start and end apart: 7, of which 6 were waited for; matrix products, arithmetic and copies ran while one was open for 2% of the time, Pallas kernels for 0%

commit v1 on v0

v1 whole, which is shorter than its diff:
```python
import jax
import jax.numpy as jnp
from jax import lax
from jax.experimental import pallas as pl
from jax.experimental.pallas import tpu as pltpu
from jax.sharding import PartitionSpec as P

highest = lax.Precision.HIGHEST
high = lax.Precision.HIGH
LANES = 128


def up(extent):
    return -(-extent // LANES) * LANES


def invert_kernel(matrix_ref, inverse_ref):
    order = matrix_ref.shape[0]
    rows = lax.broadcasted_iota(jnp.int32, (order, order), 0)
    cols = lax.broadcasted_iota(jnp.int32, (order, order), 1)
    matrix = matrix_ref[...]
    differs = jnp.bitwise_xor(rows, cols)

    def corner(size):
        inside = (rows > cols) & (differs >= size) & (differs < 2 * size)
        return jnp.where(inside, matrix, 0.0)

    inverse = jnp.where(rows == cols, 1.0, 0.0) - corner(1)
    size = 2
    while size < order:
        coupled = jnp.dot(corner(size), inverse, precision=highest)
        inverse = inverse - jnp.dot(inverse, coupled, precision=highest)
        size *= 2
    inverse_ref[...] = inverse


def invert_unit_lower(matrix):
    order = matrix.shape[0]
    steps = 2 * (order.bit_length() - 1)
    return pl.pallas_call(
        invert_kernel,
        out_shape=jax.ShapeDtypeStruct(matrix.shape, matrix.dtype),
        in_specs=[pl.BlockSpec(memory_space=pltpu.VMEM)],
        out_specs=pl.BlockSpec(memory_space=pltpu.VMEM),
        cost_estimate=pl.CostEstimate(
            flops=12 * steps * order**3, bytes_accessed=8 * order**2, transcendentals=0
        ),
    )(matrix)


def on_device(factor, coupling, right_side):
    row_count, blk_count = lax.axis_size("row"), lax.axis_size("blk")
    my_row = lax.axis_index("row")
    _, panel, order = factor.shape
    band, width = coupling.shape[1], right_side.shape[2]

    def owner(blk):
        return (row_count // 2 + blk % 2) % row_count

    def flat(blk, row):
        return blk * row_count + row

    def to_owner(value, row):
        route = [(flat(b, row), flat(b, owner(b))) for b in range(blk_count) if owner(b) != row]
        return lax.ppermute(value, ("blk", "row"), route)

    def from_owner(value, row):
        route = [(flat(b, owner(b)), flat(b, row)) for b in range(blk_count) if owner(b) != row]
        return lax.ppermute(value, ("blk", "row"), route)

    def between_owners(value, distance):
        route = [
            (flat(b, owner(b)), flat(b + distance, owner(b + distance)))
            for b in range(blk_count - distance)
        ]
        return lax.ppermute(value, ("blk", "row"), route)

    owners = sorted({owner(b) for b in range(blk_count)})

    rows = factor[0]
    first_col = my_row * panel
    diagonal = lax.dynamic_slice_in_dim(rows, first_col, panel, 1)
    base = invert_unit_lower(diagonal)
    scaled = jnp.dot(base, jnp.concatenate([right_side[0], rows], 1), precision=high)
    head = width + up(panel)
    message = jnp.concatenate(
        [scaled[:, :width], jnp.pad(base, ((0, 0), (0, up(panel) - panel))), scaled[:, width:]], 1
    )

    arrived = {}
    for k in sorted(range(row_count), key=lambda k: (k in owners, -k)):
        piece = message[:, : head + up(k * panel)]
        got = to_owner(piece, k)
        arrived[k] = jnp.where(my_row == k, piece, got) if k in owners else got

    solved = jnp.zeros((order, width + order), jnp.float32)
    sent = []
    for k in range(row_count):
        direct, base_k, weights = (
            arrived[k][:, :width],
            arrived[k][:, width : width + panel],
            arrived[k][:, head : head + k * panel],
        )
        done = k * panel
        if k:
            product = jnp.dot(weights, solved[:done, : width + done], precision=high)
            direct = direct - product[:, :width]
            left = [direct, -product[:, width:], base_k]
        else:
            left = [direct, base_k]
        ahead = up(done + panel) - done - panel
        new_rows = jnp.concatenate(left + [jnp.zeros((panel, ahead), jnp.float32)] * bool(ahead), 1)
        solved = lax.dynamic_update_slice(solved, new_rows, (done, 0))
        sent.append(new_rows[:, width:])

    scattered = [from_owner(sent[k], k) for k in range(row_count)]

    direct = solved[:, :width]
    gain = -jnp.dot(solved[:, width : width + band], coupling[0], precision=highest)
    tail_map = jnp.concatenate([direct[order - band :], gain[order - band :]], 1)
    earlier = [between_owners(tail_map, s) for s in range(1, blk_count)]
    tail = jnp.zeros((band, width), jnp.float32)
    for piece in reversed(earlier):
        tail = piece[:, :width] + jnp.dot(piece[:, width:], tail, precision=highest)
    result = direct + jnp.dot(gain, tail, precision=highest)

    pieces = [result[k * panel : (k + 1) * panel] for k in range(row_count)]
    returned = [from_owner(pieces[k], k) for k in range(row_count)]

    def finish(k):
        mine = k in owners

        def run(operands):
            scattered, returned, sent, pieces = operands
            own = scattered[k], returned[k]
            if mine:
                is_owner = owner_here
                own = (
                    jnp.where(is_owner, sent[k], own[0]),
                    jnp.where(is_owner, pieces[k], own[1]),
                )
            padded = jnp.pad(own[0], ((0, 0), (0, order - own[0].shape[1])))
            return padded[None], own[1][None]

        return run

    my_blk = lax.axis_index("blk")
    owner_here = (row_count // 2 + my_blk % 2) % row_count == my_row
    return lax.switch(
        my_row, [finish(k) for k in range(row_count)], (scattered, returned, sent, pieces)
    )


def solution(mesh):
    in_specs = (P("blk", "row", None), P("blk", None, None), P("blk", "row", None))
    out_specs = (P("blk", "row", None), P("blk", "row", None))
    return jax.shard_map(
        on_device, mesh=mesh, in_specs=in_specs, out_specs=out_specs, check_vma=False
    )
```

time: 349 us -> 153 us (0.44)
  blocking collectives: 135 us -> 0 us
  waiting for transfers between devices: 130 us -> 37.3 us
  starting transfers between devices: 8.58 us -> 35.2 us
  local copies, waits for them, and re-layouts: 12.5 us -> 29.4 us
  other arithmetic: 29.1 us -> 12.8 us
  between operations: 14.5 us -> 1.37 us
  matrix products: 16 us -> 27.7 us
  Pallas kernels: 0 us -> 7.68 us
    all_gather x3 -> x0, blocking collectives: 135 us -> none  [the longest x1 123 us: on_device(): lax.all_gather(right_side, 'row', axis=1, tiled=True)]
    psum x1 -> x0, waiting for transfers between devices: 71.4 us -> none  [from_root(): return lax.psum(jnp.where(mine, value, jnp.zeros_like(value)), axis)]
    ppermute x6 -> x27, starting transfers between devices: 8.54 us -> 35.2 us  [the longest x16 17.5 us: from_owner(): return lax.ppermute(value, ('blk', 'row'), route)]
    ppermute x6 -> x27, waiting for transfers between devices: 58.2 us -> 37.3 us  [the longest x16 37.2 us: from_owner(): return lax.ppermute(value, ('blk', 'row'), route)]
    another operation x8 -> x0, other arithmetic: 20.9 us -> none  [unit_solve(): jax.scipy.linalg.solve_triangular(matrix, target, trans=transposed, lower...]
    dot_general x14 -> x13, matrix products: 15.1 us -> 27.7 us  [the longest x7 21.6 us: on_device(): product = jnp.dot(weights, solved[:done, :width + done], precision=high)]
    slice x2 -> x21, local copies, waits for them, and re-layouts: 0.01 us -> 11.9 us  [the longest x7 6.28 us: on_device(): piece = message[:, :head + up(k * panel)]]
    select_n x3 -> x0, local copies, waits for them, and re-layouts: 10.4 us -> none  [on_device(): jnp.where(is_lower, lax.dynamic_update_slice_in_dim(inverse, new_rows, gr...]
  transfers between devices with their start and end apart: 7 -> 27, of which waited for: 6 -> 1; matrix products, arithmetic and copies ran while one was open for 2% -> 39% of each run, Pallas kernels for 0% -> 0%
where the time goes in v1:
time: 153 us; the launch traced here: 151 us
  waiting for transfers between devices  37.3 us (24%)
  starting transfers between devices  35.2 us (23%)
  local copies, waits for them, and re-layouts  29.4 us (19%)
  matrix products  27.7 us (18%)
  other arithmetic  12.8 us (8%)
  Pallas kernels  7.68 us (5%)
    ppermute x16, waiting for transfers between devices, from_owner(): return lax.ppermute(value, ('blk', 'row'), route)  37.2 us
    dot_general x7, matrix products, on_device(): product = jnp.dot(weights, solved[:done, :width + done], precision=high)  21.6 us
    ppermute x16, starting transfers between devices, from_owner(): return lax.ppermute(value, ('blk', 'row'), route)  17.5 us
    ppermute x8, starting transfers between devices, to_owner(): return lax.ppermute(value, ('blk', 'row'), route)  15.7 us
    pallas_call x1, Pallas kernels, invert_unit_lower(): pl.pallas_call(invert_kernel, out_shape=jax.ShapeDtypeStruct(matrix.shape...  7.68 us
    slice x7, local copies, waits for them, and re-layouts, on_device(): piece = message[:, :head + up(k * panel)]  6.28 us
    concatenate x7, other arithmetic, on_device(): jnp.concatenate(left + [jnp.zeros((panel, ahead), jnp.float32)] * bool(ah...  5.95 us
    dynamic_update_slice x5, local copies, waits for them, and re-layouts, on_device(): solved = lax.dynamic_update_slice(solved, new_rows, (done, 0))  5.03 us
  transfers between devices with their start and end apart: 27, of which 1 were waited for; matrix products, arithmetic and copies ran while one was open for 39% of the time, Pallas kernels for 0%

profile of v1, /device:TPU:30, one launch (start us, length us, event | category | flops | bytes accessed | tf_op | source)
XLA Modules:
  0.0 151.5 jit_solution(107831279563620203)
XLA Ops:
  0.7 1.8 %dynamic-slice_bitcast_fusion.matrix_ref = f32[192,192]{1,0:T(8,128)} fusion(f32[1,192,1536]{2,1,0:T(8,128)} %param.11, s32[]{:T(128)S(6)} %select_n.58), kind=kLoop, calls=%fused_computation.52 | loop fusion | bytes 294916 | tf_op jit(solution)/shard_map/dynamic_slice | solution.py:82
  2.4 7.7 %shard_map.50 = f32[192,192]{1,0:T(8,128)} custom-call(f32[192,192]{1,0:T(8,128)} %dynamic-slice_bitcast_fusion.matrix_ref), custom_call_target="tpu_custom_call" | custom-call | flops 1189085184 | bytes 294912 | tf_op jit(solution)/shard_map/pallas_call | solution.py:40
  10.1 0.9 pad.34
  11.1 1.7 %fusion.10 = f32[192,1664]{1,0:T(8,128)S(1)} fusion(f32[192,192]{1,0:T(8,128)} %shard_map.50, f32[192,1536]{1,0:T(8,128)S(1)} %bitcast.11, f32[192,128]{1,0:T(8,128)S(1)} %bitcast.13), kind=kOutput, calls=%fused_computation.16 | convolution fusion | flops 368369664 | bytes 2703360 | tf_op jit(solution)/shard_map/dot_general | solution.py:84
  12.8 1.4 collective-permute-start
  14.4 0.9 slice.307
  15.3 1.5 collective-permute-start.2
  16.8 1.5 collective-permute-start.3
  18.3 1.0 slice.321
  19.2 1.6 %collective-permute-start.4 = (f32[192,1024]{1,0:T(8,128)}, f32[192,1024]{1,0:T(8,128)}, u32[]{:S(2)}, u32[]{:S(2)}) collective-permute-start(f32[192,1024]{1,0:T(8,128)} %slice.321), channel_id=1, source_target_pairs={{3,4},{11,13},{19,20},{27,29}} | collective-permute-start | bytes 2359304 | tf_op jit(solution)/shard_map/ppermute | solution.py:65
  20.8 1.0 slice.328
  21.8 0.7 collective-permute-start.5
  22.5 1.1 slice.335
  23.6 1.1 slice.342
  24.8 1.2 slice.349
  25.9 1.7 %collective-permute-start.6 = (f32[192,1408]{1,0:T(8,128)}, f32[192,1408]{1,0:T(8,128)}, u32[]{:S(2)}, u32[]{:S(2)}) collective-permute-start(f32[192,1408]{1,0:T(8,128)} %slice.335), channel_id=1, source_target_pairs={{5,4},{21,20}} | collective-permute-start | bytes 3244040 | tf_op jit(solution)/shard_map/ppermute | solution.py:65
  27.6 1.0 broadcast_select_fusion.6
  29.9 1.7 %collective-permute-start.7 = (f32[192,1536]{1,0:T(8,128)}, f32[192,1536]{1,0:T(8,128)}, u32[]{:S(2)}, u32[]{:S(2)}) collective-permute-start(f32[192,1536]{1,0:T(8,128)} %slice.342), channel_id=1, source_target_pairs={{6,4},{14,13},{22,20},{30,29}} | collective-permute-start | bytes 3538952 | tf_op jit(solution)/shard_map/ppermute | solution.py:65
  31.6 1.2 fusion.23
  32.9 0.9 slice.313
  33.9 0.8 pad_maximum_fusion.7
  34.7 0.9 slice_subtract_fusion.6
  35.7 5.8 %collective-permute-start.8 = (f32[192,1792]{1,0:T(8,128)}, f32[192,1792]{1,0:T(8,128)}, u32[]{:S(2)}, u32[]{:S(2)}) collective-permute-start(f32[192,1792]{1,0:T(8,128)} %slice.349), channel_id=1, source_target_pairs={{7,4},{15,13},{23,20},{31,29}} | collective-permute-start | bytes 4128776 | tf_op jit(solution)/shard_map/ppermute | solution.py:65
  41.5 1.5 fusion.18
  43.0 0.9 slice.320
  44.0 0.9 pad_maximum_fusion.5
  44.9 0.9 slice_subtract_fusion.5
  45.9 1.3 collective-permute-start.1
  47.2 2.0 %fusion.8 = f32[192,704]{1,0:T(8,128)S(1)} fusion(f32[1536,1664]{1,0:T(8,128)S(1)} %maximum_dynamic-update-slice_fusion.1, f32[192,1024]{1,0:T(8,128)} %collective-permute-done.4), kind=kOutput, calls=%fused_computation.13 | convolution fusion | flops 467140608 | bytes 2801664 | tf_op jit(solution)/shard_map/dot_general | solution.py:106
  49.3 0.9 slice.327
  50.2 1.0 pad_maximum_fusion.4
  51.2 0.9 slice_subtract_fusion.4
  52.2 1.9 %collective-permute-start.13 = (f32[192,384]{1,0:T(8,128)}, f32[192,384]{1,0:T(8,128)}, u32[]{:S(2)}, u32[]{:S(2)}) collective-permute-start(f32[192,384]{1,0:T(8,128)} %pad_maximum_fusion.7), channel_id=1, source_target_pairs={{4,1},{13,9},{20,17},{29,25}} | collective-permute-start | bytes 884744 | tf_op jit(solution)/shard_map/ppermute | solution.py:69
  54.2 2.1 %copy-done.1 = f32[1536,1664]{1,0:T(8,128)} copy-done((f32[1536,1664]{1,0:T(8,128)}, f32[1536,1664]{1,0:T(8,128)S(1)}, u32[]{:S(2)}) %copy-start.1) | copy-done | bytes 10223640
  56.3 1.3 fusion.6
  57.8 1.0 pad_maximum_fusion.3
  58.8 1.0 constant_dynamic-update-slice_fusion.3
  59.9 1.5 collective-permute-start.15
  61.3 1.3 broadcast_select_fusion.4
  62.7 4.2 %fusion.4 = f32[192,1088]{1,0:T(8,128)S(1)} fusion(f32[1536,1664]{1,0:T(8,128)} %constant_dynamic-update-slice_fusion.3, f32[192,1408]{1,0:T(8,128)S(1)} %broadcast_select_fusion.4), kind=kOutput, calls=%fused_computation.8 | convolution fusion | flops 1203240960 | bytes 6045696 | tf_op jit(solution)/shard_map/dot_general | solution.py:106
  67.3 1.1 constant_dynamic-update-slice_fusion.2
  68.3 1.5 collective-permute-start.17
  69.8 0.9 slice.348
  70.8 5.3 %fusion.2 = f32[192,1280]{1,0:T(8,128)S(1)} fusion(f32[1536,1664]{1,0:T(8,128)} %constant_dynamic-update-slice_fusion.2, f32[192,1536]{1,0:T(8,128)} %collective-permute-done.7), kind=kOutput, calls=%fused_computation.6 | convolution fusion | flops 1698693120 | bytes 7766016 | tf_op jit(solution)/shard_map/dot_general | solution.py:106
  76.1 1.2 concatenate.75
  77.3 0.9 slice_subtract_fusion.1
  78.6 1.2 constant_dynamic-update-slice_fusion.1
  79.7 6.1 %fusion = f32[192,1472]{1,0:T(8,128)S(1)} fusion(f32[1536,1664]{1,0:T(8,128)} %constant_dynamic-update-slice_fusion.1, f32[192,1792]{1,0:T(8,128)} %collective-permute-done.8), kind=kOutput, calls=%fused_computation.4 | convolution fusion | flops 2279079936 | bytes 10469376 | tf_op jit(solution)/shard_map/dot_general | solution.py:106
  85.9 0.9 slice_subtract_fusion
  87.5 0.9 slice.355
  88.4 1.0 concatenate.68
  89.5 1.1 constant_dynamic-update-slice_fusion
  90.6 1.9 %convolution_negate_fusion = f32[1536,128]{1,0:T(8,128)S(1)} fusion(f32[1536,1664]{1,0:T(8,128)} %constant_dynamic-update-slice_fusion, f32[1,128,128]{2,1,0:T(8,128)S(1)} %copy-done), kind=kOutput, calls=%fused_computation.12 | convolution fusion | flops 302186496 | bytes 1638400 | tf_op jit(solution)/shard_map/dot_general | solution.py:119
  93.3 1.2 pad_maximum_fusion.1
  96.2 1.9 %collective-permute-start.23 = (f32[192,1408]{1,0:T(8,128)}, f32[192,1408]{1,0:T(8,128)}, u32[]{:S(2)}, u32[]{:S(2)}) collective-permute-start(f32[192,1408]{1,0:T(8,128)} %concatenate.75), channel_id=1, source_target_pairs={{4,6},{13,14},{20,22},{29,30}} | collective-permute-start | bytes 3244040 | tf_op jit(solution)/shard_map/ppermute | solution.py:69
  98.3 1.3 collective-permute-start.25
  99.6 1.9 %slice_add_fusion = f32[1536,128]{1,0:T(8,128)S(1)} fusion(f32[1536,1664]{1,0:T(8,128)} %constant_dynamic-update-slice_fusion, f32[1536,128]{1,0:T(8,128)S(1)} %convolution_negate_fusion, f32[128,128]{1,0:T(8,128)S(1)} %fusion.30, f32[128,256]{1,0:T(8,128)S(1)} %collective-permute-done.9), kind=kOutput, calls=%fused_computation.27 | convolution fusion | flops 302202880 | bytes 2490368 | tf_op jit(solution)/shard_map/dot_general | solution.py:125
  101.5 1.5 %collective-permute-start.19 = (f32[192,1024]{1,0:T(8,128)S(1)}, f32[192,1024]{1,0:T(8,128)}, u32[]{:S(2)}, u32[]{:S(2)}) collective-permute-start(f32[192,1024]{1,0:T(8,128)S(1)} %copy-done.2), channel_id=1, source_target_pairs={{13,12},{29,28}} | collective-permute-start | bytes 2359304 | tf_op jit(solution)/shard_map/ppermute | solution.py:69
  103.1 0.7 collective-permute-start.21
  108.7 1.3 collective-permute-start.26
  110.1 37.2 %collective-permute-done.26 = f32[192,128]{1,0:T(8,128)S(1)} collective-permute-done((f32[192,128]{1,0:T(8,128)S(1)}, f32[192,128]{1,0:T(8,128)S(1)}, u32[]{:S(2)}, u32[]{:S(2)}) %collective-permute-start.26) | collective-permute-done | bytes 98336 | tf_op jit(solution)/shard_map/ppermute | solution.py:69
  147.3 2.6 %conditional.1 = (f32[192,1536]{1,0:T(8,128)S(1)}, f32[192,128]{1,0:T(8,128)}) conditional(s32[]{:T(128)} %clamp.3, (f32[192,256]{1,0:T(8,128)}, f32[192,128]{1,0:T(8,128)}) %tuple.74, (f32[192,384]{1,0:T(8,128)}, f32[192,128]{1,0:T(8,128)S(1)}) %tuple.40, (f32[192,640]{1,0:T(8,128)}, ...), branch_computations={%region_0.1_spmd, %region_1.2_spmd, %region_2.3_spmd, %region_3.4_... | conditional | flops 245760 | bytes 5406770 | solution.py:149
  147.9 1.3 copy.28
  149.9 1.6 %copy.31 = f32[1,192,128]{2,1,0:T(8,128)} copy(f32[1,192,128]{2,1,0:T(8,128)} %bitcast.14) | data formatting | bytes 196608
  (97 shorter events, 12.5 us)
Async XLA Ops:
  0.6 90.0 %copy-start = (f32[1,128,128]{2,1,0:T(8,128)S(1)}, f32[1,128,128]{2,1,0:T(8,128)}, u32[]{:S(2)}) copy-start(f32[1,128,128]{2,1,0:T(8,128)} %param.12) | copy-start | bytes 196612
  2.4 8.6 %copy-start.3 = (f32[1,192,1536]{2,1,0:T(8,128)S(1)}, f32[1,192,1536]{2,1,0:T(8,128)}, u32[]{:S(2)}) copy-start(f32[1,192,1536]{2,1,0:T(8,128)} %param.11) | copy-start | bytes 3538948
  2.4 8.6 %copy-start.6 = (f32[1,192,128]{2,1,0:T(8,128)S(1)}, f32[1,192,128]{2,1,0:T(8,128)}, u32[]{:S(2)}) copy-start(f32[1,192,128]{2,1,0:T(8,128)} %param.13) | copy-start | bytes 294916
  12.8 13.2 %collective-permute-start = (f32[192,384]{1,0:T(8,128)S(1)}, f32[192,384]{1,0:T(8,128)}, u32[]{:S(2)}, u32[]{:S(2)}) collective-permute-start(f32[192,384]{1,0:T(8,128)S(1)} %pad_maximum_fusion.6), channel_id=1, source_target_pairs={{0,4},{8,13},{16,20},{24,29}} | collective-permute-start | bytes 884744 | tf_op jit(solution)/shard_map/ppermute | solution.py:65
  15.3 14.7 %collective-permute-start.2 = (f32[192,640]{1,0:T(8,128)}, f32[192,640]{1,0:T(8,128)}, u32[]{:S(2)}, u32[]{:S(2)}) collective-permute-start(f32[192,640]{1,0:T(8,128)} %slice.307), channel_id=1, source_target_pairs={{1,4},{9,13},{17,20},{25,29}} | collective-permute-start | bytes 1474568 | tf_op jit(solution)/shard_map/ppermute | solution.py:65
  16.8 18.9 %collective-permute-start.3 = (f32[192,768]{1,0:T(8,128)S(1)}, f32[192,768]{1,0:T(8,128)}, u32[]{:S(2)}, u32[]{:S(2)}) collective-permute-start(f32[192,768]{1,0:T(8,128)S(1)} %slice.314), channel_id=1, source_target_pairs={{2,4},{10,13},{18,20},{26,29}} | collective-permute-start | bytes 1769480 | tf_op jit(solution)/shard_map/ppermute | solution.py:65
  19.2 26.6 %collective-permute-start.4 = (f32[192,1024]{1,0:T(8,128)}, f32[192,1024]{1,0:T(8,128)}, u32[]{:S(2)}, u32[]{:S(2)}) collective-permute-start(f32[192,1024]{1,0:T(8,128)} %slice.321), channel_id=1, source_target_pairs={{3,4},{11,13},{19,20},{27,29}} | collective-permute-start | bytes 2359304 | tf_op jit(solution)/shard_map/ppermute | solution.py:65
  21.8 30.4 %collective-permute-start.5 = (f32[192,1152]{1,0:T(8,128)}, f32[192,1152]{1,0:T(8,128)S(1)}, u32[]{:S(2)}, u32[]{:S(2)}) collective-permute-start(f32[192,1152]{1,0:T(8,128)} %slice.328), channel_id=1, source_target_pairs={{12,13},{28,29}} | collective-permute-start | bytes 2654216 | tf_op jit(solution)/shard_map/ppermute | solution.py:65
  24.8 2.8 %copy-start.18 = (pred[384]{0:T(512)(128)(4,1)S(1)}, pred[384]{0:T(512)(128)(4,1)}, u32[]{:S(2)}) copy-start(pred[384]{0:T(512)(128)(4,1)} %constant.67.clone.1) | copy-start | bytes 1156
  25.9 33.9 %collective-permute-start.6 = (f32[192,1408]{1,0:T(8,128)}, f32[192,1408]{1,0:T(8,128)}, u32[]{:S(2)}, u32[]{:S(2)}) collective-permute-start(f32[192,1408]{1,0:T(8,128)} %slice.335), channel_id=1, source_target_pairs={{5,4},{21,20}} | collective-permute-start | bytes 3244040 | tf_op jit(solution)/shard_map/ppermute | solution.py:65
  29.9 38.4 %collective-permute-start.7 = (f32[192,1536]{1,0:T(8,128)}, f32[192,1536]{1,0:T(8,128)}, u32[]{:S(2)}, u32[]{:S(2)}) collective-permute-start(f32[192,1536]{1,0:T(8,128)} %slice.342), channel_id=1, source_target_pairs={{6,4},{14,13},{22,20},{30,29}} | collective-permute-start | bytes 3538952 | tf_op jit(solution)/shard_map/ppermute | solution.py:65
  35.7 44.0 %collective-permute-start.8 = (f32[192,1792]{1,0:T(8,128)}, f32[192,1792]{1,0:T(8,128)}, u32[]{:S(2)}, u32[]{:S(2)}) collective-permute-start(f32[192,1792]{1,0:T(8,128)} %slice.349), channel_id=1, source_target_pairs={{7,4},{15,13},{23,20},{31,29}} | collective-permute-start | bytes 4128776 | tf_op jit(solution)/shard_map/ppermute | solution.py:65
  45.9 52.4 %collective-permute-start.1 = (f32[192,256]{1,0:T(8,128)}, f32[192,256]{1,0:T(8,128)}, u32[]{:S(2)}, u32[]{:S(2)}) collective-permute-start(f32[192,256]{1,0:T(8,128)} %slice.305), channel_id=1, source_target_pairs={{4,0},{13,8},{20,16},{29,24}} | collective-permute-start | bytes 589832 | tf_op jit(solution)/shard_map/ppermute | solution.py:69
  52.2 4.1 %copy-start.1 = (f32[1536,1664]{1,0:T(8,128)}, f32[1536,1664]{1,0:T(8,128)S(1)}, u32[]{:S(2)}) copy-start(f32[1536,1664]{1,0:T(8,128)S(1)} %maximum_dynamic-update-slice_fusion) | copy-start | bytes 30670852
  52.2 49.3 %collective-permute-start.13 = (f32[192,384]{1,0:T(8,128)}, f32[192,384]{1,0:T(8,128)}, u32[]{:S(2)}, u32[]{:S(2)}) collective-permute-start(f32[192,384]{1,0:T(8,128)} %pad_maximum_fusion.7), channel_id=1, source_target_pairs={{4,1},{13,9},{20,17},{29,25}} | collective-permute-start | bytes 884744 | tf_op jit(solution)/shard_map/ppermute | solution.py:69
  59.9 43.2 %collective-permute-start.15 = (f32[192,640]{1,0:T(8,128)}, f32[192,640]{1,0:T(8,128)}, u32[]{:S(2)}, u32[]{:S(2)}) collective-permute-start(f32[192,640]{1,0:T(8,128)} %pad_maximum_fusion.5), channel_id=1, source_target_pairs={{4,2},{13,10},{20,18},{29,26}} | collective-permute-start | bytes 1474568 | tf_op jit(solution)/shard_map/ppermute | solution.py:69
  68.3 35.5 %collective-permute-start.17 = (f32[192,768]{1,0:T(8,128)}, f32[192,768]{1,0:T(8,128)}, u32[]{:S(2)}, u32[]{:S(2)}) collective-permute-start(f32[192,768]{1,0:T(8,128)} %pad_maximum_fusion.4), channel_id=1, source_target_pairs={{4,3},{13,11},{20,19},{29,27}} | collective-permute-start | bytes 1769480 | tf_op jit(solution)/shard_map/ppermute | solution.py:69
  86.8 0.6 copy-start.5
  90.6 2.0 %slice-start = ((f32[192,128]{1,0:T(8,128)}), f32[128,128]{1,0:T(8,128)S(1)}, s32[]{:S(2)}) async-start(f32[192,128]{1,0:T(8,128)} %copy-done.5), calls=%async_computation | async-start | bytes 131072 | tf_op jit(solution)/shard_map/slice | solution.py:120
  92.6 1.8 %collective-permute-start.11 = (f32[128,256]{1,0:T(8,128)S(1)}, f32[128,256]{1,0:T(8,128)S(1)}, u32[]{:S(2)}, u32[]{:S(2)}) collective-permute-start(f32[128,256]{1,0:T(8,128)S(1)} %pad_maximum_fusion.8), channel_id=1, source_target_pairs={{4,29}} | collective-permute-start | bytes 393224 | tf_op jit(solution)/shard_map/ppermute | solution.py:76
  94.4 0.9 collective-permute-start.10
  95.3 0.9 collective-permute-start.9
  96.2 5.3 %copy-start.2 = (f32[192,1024]{1,0:T(8,128)S(1)}, f32[192,1024]{1,0:T(8,128)}, u32[]{:S(2)}) copy-start(f32[192,1024]{1,0:T(8,128)} %pad_maximum_fusion.3) | copy-start | bytes 2359300
  96.2 13.9 %collective-permute-start.23 = (f32[192,1408]{1,0:T(8,128)}, f32[192,1408]{1,0:T(8,128)}, u32[]{:S(2)}, u32[]{:S(2)}) collective-permute-start(f32[192,1408]{1,0:T(8,128)} %concatenate.75), channel_id=1, source_target_pairs={{4,6},{13,14},{20,22},{29,30}} | collective-permute-start | bytes 3244040 | tf_op jit(solution)/shard_map/ppermute | solution.py:69
  98.3 49.0 %collective-permute-start.25 = (f32[192,1536]{1,0:T(8,128)}, f32[192,1536]{1,0:T(8,128)}, u32[]{:S(2)}, u32[]{:S(2)}) collective-permute-start(f32[192,1536]{1,0:T(8,128)} %pad_maximum_fusion.1), channel_id=1, source_target_pairs={{4,7},{13,15},{20,23},{29,31}} | collective-permute-start | bytes 3538952 | tf_op jit(solution)/shard_map/ppermute | solution.py:69
  101.5 7.2 %collective-permute-start.19 = (f32[192,1024]{1,0:T(8,128)S(1)}, f32[192,1024]{1,0:T(8,128)}, u32[]{:S(2)}, u32[]{:S(2)}) collective-permute-start(f32[192,1024]{1,0:T(8,128)S(1)} %copy-done.2), channel_id=1, source_target_pairs={{13,12},{29,28}} | collective-permute-start | bytes 2359304 | tf_op jit(solution)/shard_map/ppermute | solution.py:69
  103.1 7.0 %collective-permute-start.21 = (f32[192,1152]{1,0:T(8,128)S(1)}, f32[192,1152]{1,0:T(8,128)S(1)}, u32[]{:S(2)}, u32[]{:S(2)}) collective-permute-start(f32[192,1152]{1,0:T(8,128)S(1)} %pad_maximum_fusion.2), channel_id=1, source_target_pairs={{4,5},{20,21}} | collective-permute-start | bytes 2654216 | tf_op jit(solution)/shard_map/ppermute | solution.py:69
  103.9 0.7 collective-permute-start.12
  104.6 4.2 %copy-start.13 = (f32[192,128]{1,0:T(8,128)}, f32[192,128]{1,0:T(8,128)S(1)}, u32[]{:S(2)}) copy-start(f32[192,128]{1,0:T(8,128)S(1)} %collective-permute-done.12) | copy-start | bytes 294916
  104.6 0.7 collective-permute-start.14
  105.2 0.7 collective-permute-start.16
  105.9 0.7 collective-permute-start.18
  106.6 0.7 collective-permute-start.20
  107.3 0.7 copy-start.14
  107.3 0.7 collective-permute-start.22
  108.0 0.7 copy-start.16
  108.0 2.0 %collective-permute-start.24 = (f32[192,128]{1,0:T(8,128)S(1)}, f32[192,128]{1,0:T(8,128)S(1)}, u32[]{:S(2)}, u32[]{:S(2)}) collective-permute-start(f32[192,128]{1,0:T(8,128)S(1)} %get-tuple-element.71), channel_id=1, source_target_pairs={{4,6},{13,14},{20,22},{29,30}} | collective-permute-start | bytes 294920 | tf_op jit(solution)/shard_map/ppermute | solution.py:69
  108.7 38.6 %collective-permute-start.26 = (f32[192,128]{1,0:T(8,128)S(1)}, f32[192,128]{1,0:T(8,128)S(1)}, u32[]{:S(2)}, u32[]{:S(2)}) collective-permute-start(f32[192,128]{1,0:T(8,128)S(1)} %get-tuple-element.70), channel_id=1, source_target_pairs={{4,7},{13,15},{20,23},{29,31}} | collective-permute-start | bytes 294920 | tf_op jit(solution)/shard_map/ppermute | solution.py:69
  147.3 0.6 copy-start.11
  147.9 1.3 copy-start.12
  149.9 1.6 %copy-start.4 = (f32[192,1536]{1,0:T(8,128)}, f32[192,1536]{1,0:T(8,128)S(1)}, u32[]{:S(2)}) copy-start(f32[192,1536]{1,0:T(8,128)S(1)} %get-tuple-element.68) | copy-start | bytes 3538948

commit v2 on v1

v2 whole, which is shorter than its diff:
```python
import functools

import jax
import jax.numpy as jnp
from jax import lax
from jax.experimental import pallas as pl
from jax.experimental.pallas import tpu as pltpu
from jax.sharding import PartitionSpec as P

highest = lax.Precision.HIGHEST
high = lax.Precision.HIGH
LANES = 128
MIB = 1 << 20
SOLVE_LIMIT = 40 * MIB


def up(extent):
    return -(-extent // LANES) * LANES


def split(value):
    upper = value.astype(jnp.bfloat16)
    return upper, (value - upper.astype(jnp.float32)).astype(jnp.bfloat16)


def dot3(left, right):
    def one(a, b):
        return jnp.dot(a, b, preferred_element_type=jnp.float32)

    return one(left[0], right[0]) + (one(left[0], right[1]) + one(left[1], right[0]))


class Plan:
    def __init__(self, row_count, panel, order, width):
        self.row_count, self.panel, self.order, self.width = row_count, panel, order, width
        self.pair = 2 * panel
        self.shift = panel % LANES
        self.window = up(panel + self.shift)
        self.head = width + self.window
        self.half = row_count // 2 // 2 * 2

    def offset(self, k):
        return k * self.panel % LANES

    def send_width(self, k):
        return self.head + up(k * self.panel)

    def back_width(self, k):
        return self.width + up((k + 1) * self.panel)

    def classes(self):
        owners = (self.half, self.half + 1)
        return [(k,) for k in range(self.row_count) if k not in owners] + [owners]


def message_kernel(plan, row_ref, factor_ref, right_ref, *rest):
    classes = plan.classes()
    outs, (wide, inverse_ref, message, sem) = rest[: len(classes)], rest[len(classes) :]
    panel, width, window, head = plan.panel, plan.width, plan.window, plan.head
    k = row_ref[0]
    offset = pl.multiple_of(jnp.where(k % 2 == 1, plan.shift, 0), 8)
    wide[...] = jnp.zeros_like(wide)
    wide[pl.ds(offset, panel), :width] = right_ref[0]
    wide[pl.ds(offset, panel), width : width + plan.order] = factor_ref[0]
    start = pl.multiple_of(width + k * panel - offset, LANES)
    matrix = wide[:, pl.ds(start, window)]
    rows = lax.broadcasted_iota(jnp.int32, (window, window), 0)
    cols = lax.broadcasted_iota(jnp.int32, (window, window), 1)
    matrix = jnp.where((rows > cols) & (cols >= offset), matrix, 0.0)
    differs = jnp.bitwise_xor(rows, cols)

    def corner(size):
        return jnp.where((differs >= size) & (differs < 2 * size), matrix, 0.0)

    inverse = jnp.where(rows == cols, 1.0, 0.0) - corner(1)
    size = 2
    while size < window:
        parts = split(inverse)
        coupled = dot3(split(corner(size)), parts)
        inverse = inverse - dot3(parts, split(coupled))
        size *= 2
    inverse_ref[...] = inverse
    base = inverse_ref[pl.ds(offset, panel), :]
    message[:, width:head] = base
    scaled = dot3(split(base), split(wide[:, : width + plan.order]))
    message[:, :width] = scaled[:, :width]
    longest = message.shape[1] - head
    reach = lax.broadcasted_iota(jnp.int32, (panel, longest), 1) < k * panel
    message[:, head:] = jnp.where(reach, scaled[:, width : width + longest], 0.0)
    for group, out in zip(classes, outs):
        here = k == group[0]
        for other in group[1:]:
            here = here | (k == other)

        @pl.when(here)
        def _():
            copy = pltpu.make_async_copy(message.at[:, : out.shape[1]], out, sem)
            copy.start()
            copy.wait()


def make_messages(plan, row, factor, right_side):
    panel, order, width = plan.panel, plan.order, plan.width
    widths = [max(plan.send_width(k) for k in group) for group in plan.classes()]
    full = width + order + plan.window - panel
    steps = 2 * (plan.window.bit_length() - 2)
    flops = 6 * (steps * plan.window**3 + panel * plan.window * (width + order))
    return pl.pallas_call(
        functools.partial(message_kernel, plan),
        out_shape=[jax.ShapeDtypeStruct((panel, w), jnp.float32) for w in widths],
        in_specs=[
            pl.BlockSpec(memory_space=pltpu.SMEM),
            pl.BlockSpec(memory_space=pltpu.VMEM),
            pl.BlockSpec(memory_space=pltpu.VMEM),
        ],
        out_specs=[pl.BlockSpec(memory_space=pl.ANY) for _ in widths],
        scratch_shapes=[
            pltpu.VMEM((plan.window, full), jnp.float32),
            pltpu.VMEM((plan.window, plan.window), jnp.float32),
            pltpu.VMEM((panel, max(widths)), jnp.float32),
            pltpu.SemaphoreType.DMA,
        ],
        compiler_params=pltpu.CompilerParams(vmem_limit_bytes=24 * MIB),
        cost_estimate=pl.CostEstimate(
            flops=flops, bytes_accessed=8 * panel * order, transcendentals=0
        ),
        name="messages",
    )(row, factor, right_side)


def solve_kernel(plan, first, last, parity_ref, *refs):
    panel, pair, width, window, head = plan.panel, plan.pair, plan.width, plan.window, plan.head
    refs = list(refs)
    taken = [refs.pop(0) for _ in range(2 * (last - first))]
    before = [refs.pop(0) for _ in range(2)] if first else None
    outs = [refs.pop(0) for _ in range(2 * (last - first))]
    after = refs[:2]
    odd = parity_ref[0] == 1

    def stored(j):
        source, at = (before, j) if j < first else (after, j - first)
        rows = slice(at * pair, (at + 1) * pair)
        return tuple(s[rows, : width + (j + 1) * pair] for s in source)

    for q in range(first, last):
        done = q * pair
        even_ref, odd_ref = taken[2 * (q - first)], taken[2 * (q - first) + 1]
        even_msg = even_ref[...]
        odd_msg = odd_ref[...]
        owned = 2 * q == plan.half
        if owned:
            even_msg, odd_msg = jnp.where(odd, odd_msg, even_msg), jnp.where(odd, even_msg, odd_msg)
        total = jnp.zeros((pair, width), jnp.float32)
        if q:
            weights = jnp.concatenate(
                [even_msg[:, head : head + done], odd_msg[:, head : head + done]], 0
            )
            weights = split(weights)
            for j in reversed(range(q)):
                left = tuple(w[:, j * pair : (j + 1) * pair] for w in weights)
                product = dot3(left, stored(j))
                if j == q - 1:
                    total = product
                else:
                    here = product.shape[1]
                    total = jnp.concatenate([total[:, :here] + product, total[:, here:]], 1)
        rows = (q - first) * pair

        def keep(row, value):
            for place, part in zip(after, split(value)):
                place[row : row + panel, : value.shape[1]] = part

        upper = total[:panel]
        even_row = jnp.concatenate(
            [even_msg[:, :width] - upper[:, :width]]
            + [-upper[:, width:]] * bool(q)
            + [even_msg[:, width:head]],
            1,
        )
        keep(rows, even_row)
        spare = width + done + pair - even_row.shape[1]
        for place in after:
            place[rows : rows + panel, even_row.shape[1] : width + done + pair] = jnp.zeros(
                (panel, spare), jnp.bfloat16
            )
        link = split(odd_msg[:, head + done : head + done + panel])
        extra = dot3(link, split(even_row))
        lower = total[panel:]
        lower = jnp.concatenate(
            [lower + extra[:, : width + done], extra[:, width + done :]], 1
        )
        cut = width + done + pair - window
        odd_row = jnp.concatenate(
            [
                odd_msg[:, :width] - lower[:, :width],
                -lower[:, width:cut],
                jnp.concatenate(
                    [
                        odd_msg[:, width : width + lower.shape[1] - cut] - lower[:, cut:],
                        odd_msg[:, width + lower.shape[1] - cut : head],
                    ],
                    1,
                ),
            ],
            1,
        )
        keep(rows + panel, odd_row)
        out_even, out_odd = outs[2 * (q - first)], outs[2 * (q - first) + 1]
        if owned:
            wide_even = jnp.concatenate(
                [even_row, jnp.zeros((panel, spare), jnp.float32)] if spare else [even_row], 1
            )
            out_even[...] = jnp.where(odd, odd_row, wide_even)
            out_odd[...] = jnp.where(odd, wide_even, odd_row)
        else:
            out_even[...] = even_row
            out_odd[...] = odd_row


def solve(plan, first, last, parity, messages, before):
    panel, pair, width = plan.panel, plan.pair, plan.width
    shapes = []
    for q in range(first, last):
        owned = 2 * q == plan.half
        shapes.append((panel, plan.back_width(2 * q + owned)))
        shapes.append((panel, plan.back_width(2 * q + 1)))
    kept = ((last - first) * pair, width + last * pair)
    out_shape = [jax.ShapeDtypeStruct(s, jnp.float32) for s in shapes]
    out_shape += [jax.ShapeDtypeStruct(kept, jnp.bfloat16)] * 2
    operands = [parity, *messages, *before]
    specs = [pl.BlockSpec(memory_space=pltpu.SMEM)]
    specs += [pl.BlockSpec(memory_space=pltpu.VMEM)] * (len(operands) - 1)
    flops = 0
    for q in range(first, last):
        flops += 6 * pair * pair * (q * width + pair * q * (q + 1) // 2)
        flops += 6 * panel * panel * (width + q * pair)
    flops += 6 * panel * panel * width
    moved = 4 * panel * sum(m.shape[1] for m in messages) + 4 * sum(a * b for a, b in shapes)
    outs = pl.pallas_call(
        functools.partial(solve_kernel, plan, first, last),
        out_shape=out_shape,
        in_specs=specs,
        out_specs=[pl.BlockSpec(memory_space=pltpu.VMEM)] * len(out_shape),
        compiler_params=pltpu.CompilerParams(vmem_limit_bytes=SOLVE_LIMIT),
        cost_estimate=pl.CostEstimate(flops=flops, bytes_accessed=moved, transcendentals=0),
        name=f"solve_{first}_{last}",
    )(*operands)
    return outs[:-2], outs[-2:]


def solve_plain(plan, parity, messages):
    panel, width, head, window = plan.panel, plan.width, plan.head, plan.window
    half = plan.half
    messages = list(messages)
    odd = parity[0] == 1
    own, other = messages[half], messages[half + 1]
    messages[half], messages[half + 1] = jnp.where(odd, other, own), jnp.where(odd, own, other)
    full = width + plan.order + window
    solved = jnp.zeros((plan.order, full), jnp.float32)
    backs = []
    for k in range(plan.row_count):
        done = k * panel
        start = done - plan.offset(k)
        new = jnp.pad(messages[k][:, :width], ((0, 0), (0, full - width)))
        new = new + jnp.pad(
            messages[k][:, width:head], ((0, 0), (width + start, full - width - start - window))
        )
        if k:
            weights = messages[k][:, head : head + done]
            new = new - jnp.dot(weights, solved[:done], precision=high)
        solved = lax.dynamic_update_slice(solved, new, (done, 0))
        size = plan.back_width(half + 1 if k == half else k)
        backs.append(new[:, :size])
    own, other = backs[half], backs[half + 1]
    backs[half], backs[half + 1] = jnp.where(odd, other, own), jnp.where(odd, own, other)
    return backs


def place_kernel(plan, slot_ref, *rest):
    count = plan.row_count
    backs, (out, kept, staged, sem) = rest[:count], rest[count:]
    width = plan.width
    slot = slot_ref[0]
    staged[...] = jnp.zeros_like(staged)
    for k, back in enumerate(backs):

        @pl.when(slot == k)
        def _():
            copy = pltpu.make_async_copy(back, staged.at[:, : back.shape[1]], sem)
            copy.start()
            copy.wait()

    kept[...] = staged[:, : kept.shape[1]]
    out[0] = staged[:, width : width + plan.order]


def place_rows(plan, slot, backs, band):
    panel, order, width = plan.panel, plan.order, plan.width
    full = max(width + order, max(b.shape[1] for b in backs))
    return pl.pallas_call(
        functools.partial(place_kernel, plan),
        out_shape=[
            jax.ShapeDtypeStruct((1, panel, order), jnp.float32),
            jax.ShapeDtypeStruct((panel, width + band), jnp.float32),
        ],
        in_specs=[pl.BlockSpec(memory_space=pltpu.SMEM)]
        + [pl.BlockSpec(memory_space=pl.ANY)] * len(backs),
        out_specs=[pl.BlockSpec(memory_space=pltpu.VMEM)] * 2,
        scratch_shapes=[pltpu.VMEM((panel, full), jnp.float32), pltpu.SemaphoreType.DMA],
        compiler_params=pltpu.CompilerParams(vmem_limit_bytes=16 * MIB),
        cost_estimate=pl.CostEstimate(
            flops=panel * order, bytes_accessed=12 * panel * order, transcendentals=0
        ),
        name="place",
    )(slot, *backs)


def on_device(factor, coupling, right_side):
    row_count, blk_count = lax.axis_size("row"), lax.axis_size("blk")
    my_row, my_blk = lax.axis_index("row"), lax.axis_index("blk")
    _, panel, order = factor.shape
    band, width = coupling.shape[1], right_side.shape[2]
    plan = Plan(row_count, panel, order, width)
    half = plan.half

    def owner(blk):
        return half + blk % 2

    def move(value, route):
        pairs = [
            (b * row_count + s, c * row_count + d) for (b, s), (c, d) in route if (b, s) != (c, d)
        ]
        return lax.ppermute(value, ("blk", "row"), pairs)

    def source_row(blk, group):
        return group[0] if len(group) == 1 else 2 * half + 1 - owner(blk)

    blks = range(blk_count)
    classes = plan.classes()
    parity = (my_blk % 2).astype(jnp.int32).reshape(1)
    row = my_row.astype(jnp.int32).reshape(1)
    i_own = my_row == half + my_blk % 2

    made = make_messages(plan, row, factor, right_side)
    arrived = {}
    for group, value in sorted(zip(classes, made), key=lambda item: -item[0][0]):
        route = [((b, source_row(b, group)), (b, owner(b))) for b in blks]
        got = move(value, route)
        if len(group) == 1:
            arrived[group[0]] = got
        else:
            arrived[half], arrived[half + 1] = value, got

    messages = [arrived[k] for k in range(row_count)]
    footprint = 4 * order * (width + order) + 8 * panel * sum(m.shape[1] for m in messages)
    if footprint < SOLVE_LIMIT:
        middle = half // 2 + 1
        backs, kept = solve(plan, 0, middle, parity, messages[: 2 * middle], ())
        if middle < row_count // 2:
            more, _ = solve(plan, middle, row_count // 2, parity, messages[2 * middle :], kept)
            backs = list(backs) + list(more)
    else:
        backs = solve_plain(plan, parity, messages)

    last = backs[row_count - 1]
    landed = list(backs)
    for group in sorted(classes, key=lambda g: -g[0]):
        route = [((b, owner(b)), (b, source_row(b, group))) for b in blks]
        k = group[-1]
        landed[k] = move(backs[k], route)

    direct = last[panel - band :, :width]
    gain = -jnp.dot(last[panel - band :, width : width + band], coupling[0], precision=highest)
    tail_map = jnp.concatenate([direct, gain], 1)
    earlier = [
        move(tail_map, [((b, owner(b)), (b + s, owner(b + s))) for b in range(blk_count - s)])
        for s in range(1, blk_count)
    ]
    tail = jnp.zeros((band, width), jnp.float32)
    for depth, piece in enumerate(reversed(earlier)):
        step = jnp.dot(piece[:, width:], tail, precision=highest) if depth else 0.0
        tail = piece[:, :width] + step
    pushed = jnp.dot(coupling[0], tail, precision=highest)
    spread = jnp.where(i_own, pushed, 0.0)
    for j in range(row_count // 2):
        if 2 * j != half:
            spread = spread + move(
                pushed, [((b, owner(b)), (b, 2 * j + owner(b) - half)) for b in blks]
            )
    swapped = move(
        spread,
        [
            ((b, 2 * j + b % 2), (b, 2 * j + 1 - b % 2))
            for b in blks
            for j in range(row_count // 2)
        ],
    )
    pushed = jnp.where((my_row - my_blk) % 2 == 0, spread, swapped)

    slot = jnp.where(i_own, half, jnp.where((my_row == half) | (my_row == half + 1), half + 1, my_row))
    inverse, kept = place_rows(plan, slot.astype(jnp.int32).reshape(1), landed, band)
    solution = kept[:, :width] - jnp.dot(kept[:, width:], pushed, precision=highest)
    return inverse, solution[None]


def solution(mesh):
    in_specs = (P("blk", "row", None), P("blk", None, None), P("blk", "row", None))
    out_specs = (P("blk", "row", None), P("blk", "row", None))
    return jax.shard_map(
        on_device, mesh=mesh, in_specs=in_specs, out_specs=out_specs, check_vma=False
    )
```

time: 153 us -> 135 us (0.88)
  the two profiles are of different devices: /device:TPU:30 before, /device:TPU:11 now
where the time goes in v2:
time: 135 us; the launch traced here: 134 us
  starting transfers between devices  52.4 us (39%)
  waiting for transfers between devices  43.4 us (32%)
  Pallas kernels  21.5 us (16%)
  local copies, waits for them, and re-layouts  10.6 us (8%)
  matrix products  3.5 us (3%)
  other arithmetic  1.55 us (1%)
    ppermute x21, starting transfers between devices, move(): return lax.ppermute(value, ('blk', 'row'), pairs)  52.4 us
    ppermute x21, waiting for transfers between devices, move(): return lax.ppermute(value, ('blk', 'row'), pairs)  43.4 us
    pallas_call x2, Pallas kernels, solve(): pl.pallas_call(functools.partial(solve_kernel, plan, first, last), out_sh...  13.7 us
    unnamed x30, local copies, waits for them, and re-layouts  9.74 us
    pallas_call x1, Pallas kernels, make_messages(): pl.pallas_call(functools.partial(message_kernel, plan), out_shape=[jax.Sh...  5.5 us
  transfers between devices with their start and end apart: 21, of which 2 were waited for; matrix products, arithmetic and copies ran while one was open for 2% of the time, Pallas kernels for 6%

profile of v2, /device:TPU:11, one launch (start us, length us, event | category | flops | bytes accessed | tf_op | source)
XLA Modules:
  0.0 133.8 jit_solution(3587722615178447588)
XLA Ops:
  0.6 0.0 copy-start
  0.7 1.3 copy-done.5
  2.0 0.9 copy-done.10
  2.8 5.5 %messages.1 = (f32[192,384]{1,0:T(8,128)S(1)}, f32[192,640]{1,0:T(8,128)S(1)}, f32[192,768]{1,0:T(8,128)}, f32[192,1024]{1,0:T(8,128)S(1)}, f32[192,1536]{1,0:T(...) custom-call(s32[1]{0:T(128)} %bitcast.2.row_ref, f32[1,192,1536]{2,1,0:T(8,128)S(1)} %copy-done.5, ...), custom_call_target="tpu_custom_call" | custom-call | flops 1900019712 | bytes 2359296 | tf_op jit(solution)/shard_map/messages/pallas_call | solution.py:108
  8.4 0.7 collective-permute-start.11
  9.1 0.7 collective-permute-start.1
  9.8 0.7 collective-permute-start
  10.5 1.7 %collective-permute-start.4 = (f32[192,1408]{1,0:T(8,128)S(1)}, f32[192,1408]{1,0:T(8,128)}, u32[]{:S(2)}, u32[]{:S(2)}) collective-permute-start(f32[192,1408]{1,0:T(8,128)S(1)} %get-tuple-element.25.refs_4_), channel_id=1, source_target_pairs={{5,4},{12,13},{21,20},{28,29}} | collective-permute-start | bytes 3244040 | tf_op jit(solution)/shard_map/ppermute | solution.py:333
  12.2 1.7 %collective-permute-start.10 = (f32[192,1536]{1,0:T(8,128)}, f32[192,1536]{1,0:T(8,128)}, u32[]{:S(2)}, u32[]{:S(2)}) collective-permute-start(f32[192,1536]{1,0:T(8,128)} %get-tuple-element.32), channel_id=1, source_target_pairs={{6,4},{14,13},{22,20},{30,29}} | collective-permute-start | bytes 3538952 | tf_op jit(solution)/shard_map/ppermute | solution.py:333
  13.9 0.0 collective-permute-done.refs_0_
  13.9 0.7 copy-done.8
  14.6 13.5 %collective-permute-start.3 = (f32[192,1024]{1,0:T(8,128)S(1)}, f32[192,1024]{1,0:T(8,128)}, u32[]{:S(2)}, u32[]{:S(2)}) collective-permute-start(f32[192,1024]{1,0:T(8,128)S(1)} %get-tuple-element.24), channel_id=1, source_target_pairs={{3,4},{11,13},{19,20},{27,29}} | collective-permute-start | bytes 2359304 | tf_op jit(solution)/shard_map/ppermute | solution.py:333
  28.1 0.0 collective-permute-done.1.refs_1_
  28.1 0.8 copy-done.6
  28.9 1.5 %collective-permute-start.2 = (f32[192,768]{1,0:T(8,128)}, f32[192,768]{1,0:T(8,128)}, u32[]{:S(2)}, u32[]{:S(2)}) collective-permute-start(f32[192,768]{1,0:T(8,128)} %get-tuple-element.23), channel_id=1, source_target_pairs={{2,4},{10,13},{18,20},{26,29}} | collective-permute-start | bytes 1769480 | tf_op jit(solution)/shard_map/ppermute | solution.py:333
  30.4 0.0 collective-permute-done.2.refs_2_
  30.4 12.9 %collective-permute-done.3.refs_3_ = f32[192,1024]{1,0:T(8,128)} collective-permute-done((f32[192,1024]{1,0:T(8,128)S(1)}, f32[192,1024]{1,0:T(8,128)}, u32[]{:S(2)}, u32[]{:S(2)}) %collective-permute-start.3) | collective-permute-done | bytes 786464 | tf_op jit(solution)/shard_map/ppermute | solution.py:333
  43.3 0.0 collective-permute-done.4.refs_5_
  43.3 1.0 copy-done.7
  44.3 1.0 copy-done.9
  45.3 6.4 %solve_0_3.1 = (f32[192,384]{1,0:T(8,128)S(1)}, f32[192,512]{1,0:T(8,128)S(1)}, f32[192,768]{1,0:T(8,128)}, f32[192,896]{1,0:T(8,128)}, f32[192,1280]{1,0:T(8,12...) custom-call(s32[1]{0:T(128)} %bitcast.1.parity_ref, ...), custom_call_target="tpu_custom_call" | custom-call | flops 2066743296 | bytes 8257536 | tf_op jit(solution)/shard_map/solve_0_3/pallas_call | solution.py:239
  51.7 0.0 collective-permute-done.10.refs_0_
  51.7 0.0 collective-permute-done.11.refs_1_
  51.7 7.3 %solve_3_4.1 = (f32[192,1536]{1,0:T(8,128)}, f32[192,1664]{1,0:T(8,128)}, bf16[384,1664]{1,0:T(8,128)(2,1)}, bf16[384,1664]{1,0:T(8,128)(2,1)}) custom-call(s32[1]{0:T(128)} %bitcast.1.parity_ref, f32[192,1536]{1,0:T(8,128)} %collective-permute-done.10.refs_0_, f32[192,1792]{1,0:T(8,128)S(1)} %collective-permute-done.11.refs_1_, ...), custom_call_target="tpu_custom_call" | custom-call | flops 2689597440 | bytes 5013504 | tf_op jit(solution)/shard_map/solve_3_4/pallas_call | solution.py:239
  59.0 0.8 slice.29
  59.8 1.0 convolution_negate_fusion
  60.9 0.7 collective-permute-start.15
  61.6 0.7 collective-permute-start.16
  62.2 1.6 %collective-permute-start.9 = (f32[192,1280]{1,0:T(8,128)}, f32[192,1280]{1,0:T(8,128)}, u32[]{:S(2)}, u32[]{:S(2)}) collective-permute-start(f32[192,1280]{1,0:T(8,128)} %get-tuple-element.31), channel_id=1, source_target_pairs={{4,5},{13,12},{20,21},{29,28}} | collective-permute-start | bytes 2949128 | tf_op jit(solution)/shard_map/ppermute | solution.py:333
  63.9 0.7 collective-permute-start.6
  64.6 0.7 collective-permute-start.5
  65.3 0.0 collective-permute-done.15
  65.3 0.7 collective-permute-start.14
  65.9 0.0 collective-permute-done.16
  66.0 0.7 collective-permute-start.13
  66.7 0.2 fusion.2
  66.9 0.0 collective-permute-done.14
  66.9 0.7 collective-permute-start.12
  67.7 0.2 fusion.5
  67.9 0.3 convolution_bitcast_fusion
  68.2 0.0 collective-permute-done.5.rest_0_
  68.2 0.7 copy-done.3
  68.9 0.7 collective-permute-start.17
  69.6 0.0 collective-permute-done.6.rest_1_
  69.6 0.7 copy-done.1
  70.4 1.3 collective-permute-start.18
  71.6 0.0 collective-permute-done.17
  71.7 0.7 collective-permute-start.19
  72.3 30.4 %collective-permute-done.18 = f32[128,128]{0,1:T(8,128)S(1)} collective-permute-done((f32[128,128]{0,1:T(8,128)S(1)}, f32[128,128]{0,1:T(8,128)S(1)}, u32[]{:S(2)}, u32[]{:S(2)}) %collective-permute-start.18) | collective-permute-done | bytes 65568 | tf_op jit(solution)/shard_map/ppermute | solution.py:333
  102.8 1.3 collective-permute-start.8
  104.1 0.0 collective-permute-done.19
  104.1 0.0 copy-start.14
  104.1 0.6 copy-done.14
  104.7 1.5 %collective-permute-start.7 = (f32[192,768]{1,0:T(8,128)}, f32[192,768]{1,0:T(8,128)}, u32[]{:S(2)}, u32[]{:S(2)}) collective-permute-start(f32[192,768]{1,0:T(8,128)} %get-tuple-element.28), channel_id=1, source_target_pairs={{4,2},{13,10},{20,18},{29,26}} | collective-permute-start | bytes 1769480 | tf_op jit(solution)/shard_map/ppermute | solution.py:333
  106.2 1.5 %add_add_fusion = f32[128,128]{0,1:T(8,128)} fusion(f32[128,128]{0,1:T(8,128)} %copy-done.14, f32[128,128]{0,1:T(8,128)} %copy-done.13, f32[128,128]{0,1:T(8,128)} %copy-done.12, f32[128,128]{0,1:T(8,128)} %copy-done.11, pred[]{:T(512)S(6)} %eq.16), kind=kLoop, calls=%fused_computation.16 | loop fusion | flops 65536 | bytes 327681 | tf_op jit(solution)/shard_map/add | solution.py:387
  107.7 0.0 collective-permute-done.7.rest_2_
  107.7 20.0 %collective-permute-start.20 = (f32[128,128]{0,1:T(8,128)}, f32[128,128]{0,1:T(8,128)}, u32[]{:S(2)}, u32[]{:S(2)}) collective-permute-start(f32[128,128]{0,1:T(8,128)} %add_add_fusion), channel_id=1, source_target_pairs={{0,1},{2,3},{4,5},{6,7},{9,8},{11,10},{13,12},{15,14},{16,17},{18,... | collective-permute-start | bytes 196616 | tf_op jit(solution)/shard_map/ppermute | solution.py:333
  127.8 0.0 collective-permute-done.8.rest_3_
  127.8 0.0 collective-permute-done.9.rest_5_
  127.8 0.0 collective-permute-done.13.rest_7_
  127.8 1.0 copy-done.2
  128.8 1.0 copy-done.4
  129.7 2.3 %place.1 = (f32[1,192,1536]{2,1,0:T(8,128)}, f32[192,256]{1,0:T(8,128)S(1)}) custom-call(s32[1]{0:T(128)} %bitcast.slot_ref, f32[192,384]{1,0:T(8,128)S(1)} %copy-done.4, f32[192,512]{1,0:T(8,128)S(1)} %copy-done.2, f32[192,768]{1,0:T(8,128)} %collective-permute-done.7.rest_2_, f32[192,896]{1,0:T(8,128)} %collective-permute-done.8.rest_3_, ...), custom_call_target="tpu_custom_call" | custom-call | flops 294912 | bytes 3538944 | tf_op jit(solution)/shard_map/place/pallas_call | solution.py:300
  132.0 1.8 %subtract_bitcast_fusion = f32[1,192,128]{2,1,0:T(8,128)} fusion(f32[192,256]{1,0:T(8,128)S(1)} %get-tuple-element.39, f32[128,128]{0,1:T(8,128)} %add_add_fusion, f32[128,128]{0,1:T(8,128)} %collective-permute-done.20, pred[]{:T(512)S(6)} %eq.19), kind=kOutput, calls=%fused_computation.3 | convolution fusion | flops 37789696 | bytes 425985 | tf_op jit(solution)/shard_map/dot_general | solution.py:402
  (20 shorter events, 0.0 us)
Async XLA Ops:
  0.6 59.2 %copy-start = (f32[1,128,128]{2,1,0:T(8,128)S(1)}, f32[1,128,128]{2,1,0:T(8,128)}, u32[]{:S(2)}) copy-start(f32[1,128,128]{2,1,0:T(8,128)} %param.4) | copy-start | bytes 196612
  0.7 1.3 copy-start.5
  2.0 0.9 copy-start.10
  8.4 43.3 %collective-permute-start.11 = (f32[192,1792]{1,0:T(8,128)}, f32[192,1792]{1,0:T(8,128)S(1)}, u32[]{:S(2)}, u32[]{:S(2)}) collective-permute-start(f32[192,1792]{1,0:T(8,128)} %get-tuple-element.33), channel_id=1, source_target_pairs={{7,4},{15,13},{23,20},{31,29}} | collective-permute-start | bytes 4128776 | tf_op jit(solution)/shard_map/ppermute | solution.py:333
  9.1 19.0 %collective-permute-start.1 = (f32[192,640]{1,0:T(8,128)S(1)}, f32[192,640]{1,0:T(8,128)S(1)}, u32[]{:S(2)}, u32[]{:S(2)}) collective-permute-start(f32[192,640]{1,0:T(8,128)S(1)} %get-tuple-element.22), channel_id=1, source_target_pairs={{1,4},{9,13},{17,20},{25,29}} | collective-permute-start | bytes 1474568 | tf_op jit(solution)/shard_map/ppermute | solution.py:333
  9.8 4.1 %collective-permute-start = (f32[192,384]{1,0:T(8,128)S(1)}, f32[192,384]{1,0:T(8,128)S(1)}, u32[]{:S(2)}, u32[]{:S(2)}) collective-permute-start(f32[192,384]{1,0:T(8,128)S(1)} %get-tuple-element.21), channel_id=1, source_target_pairs={{0,4},{8,13},{16,20},{24,29}} | collective-permute-start | bytes 884744 | tf_op jit(solution)/shard_map/ppermute | solution.py:333
  10.5 32.8 %collective-permute-start.4 = (f32[192,1408]{1,0:T(8,128)S(1)}, f32[192,1408]{1,0:T(8,128)}, u32[]{:S(2)}, u32[]{:S(2)}) collective-permute-start(f32[192,1408]{1,0:T(8,128)S(1)} %get-tuple-element.25.refs_4_), channel_id=1, source_target_pairs={{5,4},{12,13},{21,20},{28,29}} | collective-permute-start | bytes 3244040 | tf_op jit(solution)/shard_map/ppermute | solution.py:333
  12.2 39.5 %collective-permute-start.10 = (f32[192,1536]{1,0:T(8,128)}, f32[192,1536]{1,0:T(8,128)}, u32[]{:S(2)}, u32[]{:S(2)}) collective-permute-start(f32[192,1536]{1,0:T(8,128)} %get-tuple-element.32), channel_id=1, source_target_pairs={{6,4},{14,13},{22,20},{30,29}} | collective-permute-start | bytes 3538952 | tf_op jit(solution)/shard_map/ppermute | solution.py:333
  13.9 0.7 copy-start.8
  14.6 28.7 %collective-permute-start.3 = (f32[192,1024]{1,0:T(8,128)S(1)}, f32[192,1024]{1,0:T(8,128)}, u32[]{:S(2)}, u32[]{:S(2)}) collective-permute-start(f32[192,1024]{1,0:T(8,128)S(1)} %get-tuple-element.24), channel_id=1, source_target_pairs={{3,4},{11,13},{19,20},{27,29}} | collective-permute-start | bytes 2359304 | tf_op jit(solution)/shard_map/ppermute | solution.py:333
  28.1 0.8 copy-start.6
  28.9 1.5 %collective-permute-start.2 = (f32[192,768]{1,0:T(8,128)}, f32[192,768]{1,0:T(8,128)}, u32[]{:S(2)}, u32[]{:S(2)}) collective-permute-start(f32[192,768]{1,0:T(8,128)} %get-tuple-element.23), channel_id=1, source_target_pairs={{2,4},{10,13},{18,20},{26,29}} | collective-permute-start | bytes 1769480 | tf_op jit(solution)/shard_map/ppermute | solution.py:333
  43.3 1.0 copy-start.7
  44.3 1.0 copy-start.9
  60.9 4.4 %collective-permute-start.15 = (f32[128,256]{1,0:T(8,128)S(1)}, f32[128,256]{1,0:T(8,128)S(1)}, u32[]{:S(2)}, u32[]{:S(2)}) collective-permute-start(f32[128,256]{1,0:T(8,128)S(1)} %pad_maximum_fusion), channel_id=1, source_target_pairs={{4,20},{13,29}} | collective-permute-start | bytes 393224 | tf_op jit(solution)/shard_map/ppermute | solution.py:333
  61.6 4.4 %collective-permute-start.16 = (f32[128,256]{1,0:T(8,128)S(1)}, f32[128,256]{1,0:T(8,128)S(1)}, u32[]{:S(2)}, u32[]{:S(2)}) collective-permute-start(f32[128,256]{1,0:T(8,128)S(1)} %pad_maximum_fusion), channel_id=1, source_target_pairs={{4,29}} | collective-permute-start | bytes 393224 | tf_op jit(solution)/shard_map/ppermute | solution.py:333
  62.2 65.5 %collective-permute-start.9 = (f32[192,1280]{1,0:T(8,128)}, f32[192,1280]{1,0:T(8,128)}, u32[]{:S(2)}, u32[]{:S(2)}) collective-permute-start(f32[192,1280]{1,0:T(8,128)} %get-tuple-element.31), channel_id=1, source_target_pairs={{4,5},{13,12},{20,21},{29,28}} | collective-permute-start | bytes 2949128 | tf_op jit(solution)/shard_map/ppermute | solution.py:333
  63.9 5.7 %collective-permute-start.6 = (f32[192,512]{1,0:T(8,128)S(1)}, f32[192,512]{1,0:T(8,128)S(1)}, u32[]{:S(2)}, u32[]{:S(2)}) collective-permute-start(f32[192,512]{1,0:T(8,128)S(1)} %get-tuple-element.27), channel_id=1, source_target_pairs={{4,1},{13,9},{20,17},{29,25}} | collective-permute-start | bytes 1179656 | tf_op jit(solution)/shard_map/ppermute | solution.py:333
  64.6 3.6 %collective-permute-start.5 = (f32[192,384]{1,0:T(8,128)S(1)}, f32[192,384]{1,0:T(8,128)S(1)}, u32[]{:S(2)}, u32[]{:S(2)}) collective-permute-start(f32[192,384]{1,0:T(8,128)S(1)} %get-tuple-element.26), channel_id=1, source_target_pairs={{4,0},{13,8},{20,16},{29,24}} | collective-permute-start | bytes 884744 | tf_op jit(solution)/shard_map/ppermute | solution.py:333
  65.3 1.7 %collective-permute-start.14 = (f32[128,256]{1,0:T(8,128)S(1)}, f32[128,256]{1,0:T(8,128)S(1)}, u32[]{:S(2)}, u32[]{:S(2)}) collective-permute-start(f32[128,256]{1,0:T(8,128)S(1)} %pad_maximum_fusion), channel_id=1, source_target_pairs={{4,13},{13,20},{20,29}} | collective-permute-start | bytes 393224 | tf_op jit(solution)/shard_map/ppermute | solution.py:333
  66.0 61.8 %collective-permute-start.13 = (f32[192,1664]{1,0:T(8,128)}, f32[192,1664]{1,0:T(8,128)S(1)}, u32[]{:S(2)}, u32[]{:S(2)}) collective-permute-start(f32[192,1664]{1,0:T(8,128)} %get-tuple-element.37), channel_id=1, source_target_pairs={{4,7},{13,15},{20,23},{29,31}} | collective-permute-start | bytes 3833864 | tf_op jit(solution)/shard_map/ppermute | solution.py:333
  66.9 60.8 %collective-permute-start.12 = (f32[192,1536]{1,0:T(8,128)}, f32[192,1536]{1,0:T(8,128)S(1)}, u32[]{:S(2)}, u32[]{:S(2)}) collective-permute-start(f32[192,1536]{1,0:T(8,128)} %get-tuple-element.36), channel_id=1, source_target_pairs={{4,6},{13,14},{20,22},{29,30}} | collective-permute-start | bytes 3538952 | tf_op jit(solution)/shard_map/ppermute | solution.py:333
  68.2 3.5 %copy-start.11 = (f32[128,128]{0,1:T(8,128)}, f32[128,128]{0,1:T(8,128)S(1)}, u32[]{:S(2)}) copy-start(f32[128,128]{0,1:T(8,128)S(1)} %convolution_bitcast_fusion) | copy-start | bytes 196612
  68.2 0.7 copy-start.3
  68.9 2.7 %collective-permute-start.17 = (f32[128,128]{0,1:T(8,128)S(1)}, f32[128,128]{0,1:T(8,128)S(1)}, u32[]{:S(2)}, u32[]{:S(2)}) collective-permute-start(f32[128,128]{0,1:T(8,128)S(1)} %convolution_bitcast_fusion), channel_id=1, source_target_pairs={{4,0},{13,9},{20,16},{29,25}} | collective-permute-start | bytes 196616 | tf_op jit(solution)/shard_map/ppermute | solution.py:333
  69.6 0.8 copy-start.1
  70.4 32.4 %collective-permute-start.18 = (f32[128,128]{0,1:T(8,128)S(1)}, f32[128,128]{0,1:T(8,128)S(1)}, u32[]{:S(2)}, u32[]{:S(2)}) collective-permute-start(f32[128,128]{0,1:T(8,128)S(1)} %convolution_bitcast_fusion), channel_id=1, source_target_pairs={{4,2},{13,11},{20,18},{29,27}} | collective-permute-start | bytes 196616 | tf_op jit(solution)/shard_map/ppermute | solution.py:333
  71.7 32.4 %copy-start.12 = (f32[128,128]{0,1:T(8,128)}, f32[128,128]{0,1:T(8,128)S(1)}, u32[]{:S(2)}) copy-start(f32[128,128]{0,1:T(8,128)S(1)} %collective-permute-done.17) | copy-start | bytes 196612
  71.7 32.4 %collective-permute-start.19 = (f32[128,128]{0,1:T(8,128)S(1)}, f32[128,128]{0,1:T(8,128)S(1)}, u32[]{:S(2)}, u32[]{:S(2)}) collective-permute-start(f32[128,128]{0,1:T(8,128)S(1)} %convolution_bitcast_fusion), channel_id=1, source_target_pairs={{4,6},{13,15},{20,22},{29,31}} | collective-permute-start | bytes 196616 | tf_op jit(solution)/shard_map/ppermute | solution.py:333
  102.8 1.3 copy-start.13
  102.8 25.0 %collective-permute-start.8 = (f32[192,896]{1,0:T(8,128)}, f32[192,896]{1,0:T(8,128)}, u32[]{:S(2)}, u32[]{:S(2)}) collective-permute-start(f32[192,896]{1,0:T(8,128)} %get-tuple-element.29), channel_id=1, source_target_pairs={{4,3},{13,11},{20,19},{29,27}} | collective-permute-start | bytes 2064392 | tf_op jit(solution)/shard_map/ppermute | solution.py:333
  104.1 0.6 copy-start.14
  104.7 3.0 %collective-permute-start.7 = (f32[192,768]{1,0:T(8,128)}, f32[192,768]{1,0:T(8,128)}, u32[]{:S(2)}, u32[]{:S(2)}) collective-permute-start(f32[192,768]{1,0:T(8,128)} %get-tuple-element.28), channel_id=1, source_target_pairs={{4,2},{13,10},{20,18},{29,26}} | collective-permute-start | bytes 1769480 | tf_op jit(solution)/shard_map/ppermute | solution.py:333
  107.7 24.3 %collective-permute-start.20 = (f32[128,128]{0,1:T(8,128)}, f32[128,128]{0,1:T(8,128)}, u32[]{:S(2)}, u32[]{:S(2)}) collective-permute-start(f32[128,128]{0,1:T(8,128)} %add_add_fusion), channel_id=1, source_target_pairs={{0,1},{2,3},{4,5},{6,7},{9,8},{11,10},{13,12},{15,14},{16,17},{18,... | collective-permute-start | bytes 196616 | tf_op jit(solution)/shard_map/ppermute | solution.py:333
  127.8 1.0 copy-start.2
  128.8 1.0 copy-start.4
